TPU v7x, 32 devices: a 4x4x1 block of a 4x4x8 slice. The times are simulated.
32 devices in a mesh: dp: 1 (over z), sp: 32 (over x, y, core).
Axes of the slice: x: 4, y: 4, z: 1, core: 2. Of those that a mesh axis runs over, the one named last changes fastest.
The devices are a block of a 4x4x8 slice.
Arguments:
- q: bfloat16 [32, 20, 128], P('dp')
- k: bfloat16 [32, 8192, 20, 128], P('dp', 'sp')
- v: bfloat16 [32, 8192, 20, 128], P('dp', 'sp')
Outputs:
- q: bfloat16 [32, 20, 128], P('dp')
All inputs are finite; a program needn't handle non-finite values.
Results may differ from a plain program's by a relative error of at most 0.012.
Values are sent between devices in bfloat16 or wider.
A program may use at most 768 MiB of HBM per device.

v0:
```python
import jax
import jax.numpy as jnp
from jax import lax
from jax.sharding import PartitionSpec as P


def einsum(form, a, b):
    return jnp.einsum(form, a.astype(jnp.float32), b.astype(jnp.float32))


def part_of(q, k, v):
    grouped = q.reshape(q.shape[0], k.shape[2], -1, q.shape[2])
    scores = einsum("bgsd,bugd->bgsu", grouped, k) * q.shape[2] ** -0.5
    high = jnp.max(scores, -1, keepdims=True)
    weights = jnp.exp(scores - high)
    seen = einsum("bgsu,bugd->bgsd", weights.astype(jnp.bfloat16), v)
    return jnp.concatenate([seen, jnp.sum(weights, -1, keepdims=True), high], -1)


def together(parts):
    seen, total, high = parts[..., :-2], parts[..., -2:-1], parts[..., -1:]
    scale = jnp.exp(high - jnp.max(high, 0))
    return (jnp.sum(seen * scale, 0) / jnp.sum(total * scale, 0)).astype(jnp.bfloat16)


def solution(mesh):
    def step(q, k, v):
        return together(lax.all_gather(part_of(q, k, v), "sp")).reshape(q.shape)

    return jax.shard_map(
        step,
        mesh=mesh,
        in_specs=(P("dp", None, None), P("dp", "sp", None, None), P("dp", "sp", None, None)),
        out_specs=P("dp", None, None),
        check_vma=False,
    )
```

profile of v0, /device:TPU:97, one launch (start us, length us, event | category | flops | bytes accessed | tf_op | source)
XLA Modules:
  0.0 151.9 jit_solution(13872149622081089965)
XLA Ops:
  6.5 0.0 all-gather.3.cloned.1.call-start
  6.6 16.9 %fusion.9 = f32[32,20,1,256]{3,2,1,0:T(1,128)S(1)} fusion(bf16[32,256,20,128]{3,1,2,0:T(8,128)(2,1)} %param.4, bf16[32,20,128,1]{2,0,1,3:T(8,128)(2,1)} %bitcast.22), kind=kOutput, calls=%fused_computation.16 | convolution fusion | flops 41943040 | bytes 42762240 | tf_op jit(solution)/shard_map/bgsd,bugd->bgsu/dot_general | solution.py:8
  23.4 0.2 fusion.7
  23.6 0.3 fusion.8
  23.9 15.8 %fusion.3 = f32[32,20,1,128]{3,2,1,0:T(1,128)S(1)} fusion(bf16[32,256,20,128]{3,1,2,0:T(8,128)(2,1)} %param.5, bf16[32,20,256,1]{2,0,1,3:T(8,128)(2,1)S(1)} %get-tuple-element.7), kind=kOutput, calls=%fused_computation.9 | convolution fusion | flops 41943040 | bytes 42598400 | tf_op jit(solution)/shard_map/bgsu,bugd->bgsd/dot_general | solution.py:8
  39.7 0.2 copy.13
  40.0 0.2 copy.12
  40.2 1.0 pad_maximum_fusion
  41.2 0.1 all-gather.3.cloned.1.call-update
  41.2 81.5 %all-gather.3.cloned.1.call-done = f32[1024,20,1,130]{3,0,1,2:T(8,128)} async-done(((f32[32,20,1,130]{3,0,1,2:T(8,128)}), f32[1024,20,1,130]{3,0,1,2:T(8,128)}) %all-gather.3.cloned.1.call-update) | async-done | bytes 10649616 | tf_op jit(solution)/shard_map/all_gather | solution.py:28
  122.8 0.0 copy-start
  122.8 7.0 %slice_reduce_fusion = f32[32,20]{0,1:T(8,128)S(1)} fusion(f32[32,32,20,1,130]{4,1,0,2,3:T(8,128)} %bitcast.19), kind=kLoop, calls=%fused_computation.5 | loop fusion | flops 19840 | bytes 84480 | tf_op jit(solution)/shard_map/reduce_max | solution.py:22
  129.8 11.1 %fusion = (f32[32,20]{0,1:T(8,128)S(1)}, f32[32,32,20]{1,0,2:T(8,128)S(1)}) fusion(f32[32,32,20,1,130]{4,1,0,2,3:T(8,128)} %bitcast.20, f32[32,20]{0,1:T(8,128)S(1)} %slice_reduce_fusion), kind=kLoop, calls=%fused_computation.1 | loop fusion | flops 60800 | bytes 250880 | tf_op jit(solution)/shard_map/reduce_sum | solution.py:23
  140.9 0.0 copy-done
  140.9 3.2 %fusion.1 = f32[32,20,128]{2,0,1:T(8,128)S(1)} fusion(f32[32,32,20,1,130]{4,1,0,2,3:T(8,128)S(1)} %bitcast.21, f32[32,32,20]{1,0,2:T(8,128)S(1)} %get-tuple-element.6), kind=kLoop, calls=%fused_computation.3 | loop fusion | flops 5160960 | bytes 10895360 | tf_op jit(solution)/shard_map/reduce_sum | solution.py:23
  144.2 0.8 divide_convert_fusion
  (1 shorter events, 0.0 us)
Async XLA Ops:
  6.5 116.2 %all-gather.3.cloned.1.call-start = ((), (), s32[]{:S(2)}) async-start(), calls=%async_computation | async-start | bytes 21626880 | tf_op jit(solution)/shard_map/all_gather | solution.py:28
  122.8 18.2 %copy-start = (f32[1024,20,1,130]{3,0,1,2:T(8,128)S(1)}, f32[1024,20,1,130]{3,0,1,2:T(8,128)}, u32[]{:S(2)}) copy-start(f32[1024,20,1,130]{3,0,1,2:T(8,128)} %all-gather.3.cloned.1.call-done) | copy-start | bytes 31948804
Sparse Core Ops, SparseCore 0:
  41.3 81.3 all-gather.2
where the time goes:
time: 152 us
  waiting for transfers between devices  81.6 us (54%)
  matrix products  32.6 us (21%)
  other arithmetic  23.7 us (16%)
  between operations  13.5 us (9%)
    all_gather x1, waiting for transfers between devices, step(): return together(lax.all_gather(part_of(q, k, v), 'sp')).reshape(q.shape)  81.5 us
    dot_general x2, matrix products, einsum(): return jnp.einsum(form, a.astype(jnp.float32), b.astype(jnp.float32))  32.6 us
    reduce_sum x1, other arithmetic, together(): jnp.sum(total * scale, 0)  11.1 us
    reduce_max x1, other arithmetic, together(): scale = jnp.exp(high - jnp.max(high, 0))  7.03 us
    reduce_sum x1, other arithmetic, together(): jnp.sum(seen * scale, 0) / jnp.sum(total * scale, 0)  3.23 us
  transfers between devices with their start and end apart: 1, of which 1 were waited for; matrix products, arithmetic and copies ran while one was open for 0% of the time, Pallas kernels for 0%

commit v1 on v0

v1 whole, which is shorter than its diff:
```python
import functools
import math

import jax
import jax.numpy as jnp
from jax import lax
from jax.experimental import pallas as pl
from jax.experimental.pallas import tpu as pltpu
from jax.sharding import PartitionSpec as P

SLOTS = 4
LAG_A = 4
LAG_B = 3
F32, BF16 = jnp.float32, jnp.bfloat16


def weights_of(q, keys, slot, scale):
    rows, depth = q.shape
    half, tokens = rows // 2, keys.shape[2]
    zero = jnp.zeros((half, depth), q.dtype)
    both = jnp.concatenate([jnp.concatenate([q[:half], zero], 1), jnp.concatenate([zero, q[half:]], 1)], 0)
    lane = lax.broadcasted_iota(jnp.int32, (tokens, rows), 1) % half
    scores = jnp.zeros((tokens, rows), F32)
    for pair in range(half):
        two = jnp.concatenate([keys[slot, pair], keys[slot, pair + half]], 1)
        got = lax.dot_general(two, both, (((1,), (1,)), ((), ())), preferred_element_type=F32)
        scores = jnp.where(lane == pair, got, scores)
    scores = scores * scale
    high = jnp.max(scores, 0, keepdims=True)
    weights = jnp.exp(scores - high)
    return weights.T.astype(BF16), high, jnp.sum(weights, 0, keepdims=True)


def seen_of(weights, values, slot):
    rows, depth, block = weights.shape[0], values.shape[3], 16
    row = lax.broadcasted_iota(jnp.int32, (block, depth), 0)
    seen = []
    for first in range(0, rows, block):
        some = weights[first : first + block]
        out = jnp.zeros((block, depth), F32)
        for j in range(block):
            out = jnp.where(row == j, jnp.dot(some, values[slot, first + j], preferred_element_type=F32), out)
        seen.append(out)
    return jnp.concatenate(seen, 0)


def rows_of(stats, head, which, count):
    rows = stats.shape[-1]
    place = lax.broadcasted_iota(jnp.int32, (8, rows), 0)
    out = jnp.broadcast_to(stats[head, 0, which : which + 1], (8, rows))
    for j in range(1, count):
        out = jnp.where(place == j, jnp.broadcast_to(stats[head, j, which : which + 1], (8, rows)), out)
    return out


def together(parts, stats, head, count, last):
    rows = parts.shape[2]
    place = lax.broadcasted_iota(jnp.int32, (8, stats.shape[-1]), 0)
    high = rows_of(stats, head, 0, count)
    top = jnp.max(high, 0, keepdims=True)
    scale = jnp.where(place < count, jnp.exp(high - top), 0.0)
    total = jnp.sum(jnp.where(place < count, rows_of(stats, head, 1, count), 0.0) * scale, 0, keepdims=True)
    if last:
        scale = scale / total
    columns = scale.T[:rows]
    out = parts[head, 0].astype(F32) * columns[:, 0:1]
    for j in range(1, count):
        out = out + parts[head, j].astype(F32) * columns[:, j : j + 1]
    return out, top, total


def kernel(n, inner, q_ref, k_ref, v_ref, o_ref, keys, values, held, held_stats, parts_a, stats_a, parts_b, stats_b, k_sem, v_sem, recv_a, recv_as, recv_b, recv_bs, sent):
    heads, rows, depth = q_ref.shape
    outer = n // inner
    scale = depth**-0.5
    me = lax.axis_index("sp")
    mine_a, mine_b = lax.rem(me, inner), me // inner
    peers_a = [mine_b * inner + lax.rem(mine_a + i, inner) for i in range(1, inner)]
    peers_b = [lax.rem(mine_b + i, outer) * inner + mine_a for i in range(1, outer)]

    def fetch(ref, buffer, sem, head):
        slot = lax.rem(head, SLOTS)
        return pltpu.make_async_copy(ref.at[:, head], buffer.at[slot], sem.at[slot])

    fetch_k = functools.partial(fetch, k_ref, keys, k_sem)
    fetch_v = functools.partial(fetch, v_ref, values, v_sem)
    for head in range(SLOTS):
        fetch_k(head).start()
        fetch_v(head).start()

    barrier = pltpu.get_barrier_semaphore()
    for peer in peers_a + peers_b:
        pl.semaphore_signal(barrier, inc=1, device_id={"sp": peer}, device_id_type=pl.DeviceIdType.MESH)
    pl.semaphore_wait(barrier, len(peers_a) + len(peers_b))

    def send(parts, stats, mine, peers, head, recv, recv_s, place):
        for peer in peers:
            for ref, sem, kind in ((parts, recv, 0), (stats, recv_s, 1)):
                pltpu.make_async_remote_copy(
                    src_ref=ref.at[head, mine],
                    dst_ref=ref.at[head, mine],
                    send_sem=sent.at[place + kind],
                    recv_sem=sem.at[head],
                    device_id={"sp": peer},
                    device_id_type=pl.DeviceIdType.MESH,
                ).start()

    def arrived(parts, stats, head, recv, recv_s, count):
        for ref, sem in ((parts, recv), (stats, recv_s)):
            some = ref.at[head, 0 : count - 1]
            pltpu.make_async_copy(some, some, sem.at[head]).wait()

    def send_a(head):
        send(parts_a, stats_a, mine_a, peers_a, head, recv_a, recv_as, 0)

    def send_b(head):
        send(parts_b, stats_b, mine_b, peers_b, head, recv_b, recv_bs, 2)

    def weigh(head):
        return weights_of(q_ref[head], keys, lax.rem(head, SLOTS), scale)

    def hold(weights, high, total):
        held[...] = weights
        held_stats[0:1] = high
        held_stats[1:2] = total

    def part(head, weights, stats):
        parts_a[head, mine_a] = seen_of(weights, values, lax.rem(head, SLOTS)).astype(BF16)
        stats_a[head, mine_a] = stats

    def block(head):
        seen, top, total = together(parts_a, stats_a, head, inner, False)
        parts_b[head, mine_b] = seen.astype(BF16)
        stats_b[head, mine_b, 0:1] = top
        stats_b[head, mine_b, 1:2] = total

    def final(head, to):
        o_ref[to] = together(parts_b, stats_b, head, outer, True)[0].astype(o_ref.dtype)

    for ref in (parts_a, stats_a, parts_b, stats_b):
        ref[heads] = jnp.zeros(ref.shape[1:], ref.dtype)

    fetch_k(0).wait()
    hold(*weigh(0))
    fetch_k(SLOTS).start()

    def step(i, _):
        a = i - 1 - LAG_A
        f = a - LAG_B

        @pl.when(a >= 0)
        def _():
            arrived(parts_a, stats_a, a, recv_a, recv_as, inner)

        @pl.when(f >= 0)
        def _():
            arrived(parts_b, stats_b, f, recv_b, recv_bs, outer)

        fetch_k(i).wait()
        fetch_v(i - 1).wait()
        weights, stats = held[...], held_stats[...]
        new = weigh(i)
        part(i - 1, weights, stats)
        block(jnp.where(a >= 0, a, heads))
        final(jnp.where(f >= 0, f, heads), jnp.maximum(f, 0))
        hold(*new)
        send_a(i - 1)

        @pl.when(a >= 0)
        def _():
            send_b(a)

        @pl.when(i + SLOTS < heads)
        def _():
            fetch_k(i + SLOTS).start()

        @pl.when(i - 1 + SLOTS < heads)
        def _():
            fetch_v(i - 1 + SLOTS).start()

        return 0

    lax.fori_loop(1, heads, step, 0)
    fetch_v(heads - 1).wait()
    part(heads - 1, held[...], held_stats[...])
    send_a(heads - 1)

    def drain_a(a, _):
        arrived(parts_a, stats_a, a, recv_a, recv_as, inner)
        block(a)
        send_b(a)
        return 0

    lax.fori_loop(heads - 1 - LAG_A, heads, drain_a, 0)

    def drain_b(f, _):
        arrived(parts_b, stats_b, f, recv_b, recv_bs, outer)
        final(f, f)
        return 0

    lax.fori_loop(heads - 1 - LAG_A - LAG_B, heads, drain_b, 0)
    for place, ref, count in ((0, parts_a, inner), (1, stats_a, inner), (2, parts_b, outer), (3, stats_b, outer)):
        some = ref.at[0:heads, 0 : count - 1]
        pltpu.make_async_copy(some, some, sent.at[place]).wait()


def solution(mesh):
    n = mesh.shape["sp"]
    inner = 2 * math.isqrt(n // 2)
    outer = n // inner

    def step(q, k, v):
        q, k, v = q.transpose(1, 0, 2), k.transpose(0, 2, 1, 3), v.transpose(0, 2, 1, 3)
        heads, rows, depth = q.shape
        tokens = k.shape[2]
        ring = (SLOTS, rows, tokens, depth)
        whole = pl.BlockSpec(memory_space=pltpu.VMEM)
        out = pl.pallas_call(
            functools.partial(kernel, n, inner),
            out_shape=jax.ShapeDtypeStruct(q.shape, q.dtype),
            in_specs=[whole, pl.BlockSpec(memory_space=pl.ANY), pl.BlockSpec(memory_space=pl.ANY)],
            out_specs=whole,
            scratch_shapes=[
                pltpu.VMEM(ring, k.dtype),
                pltpu.VMEM(ring, v.dtype),
                pltpu.VMEM((rows, tokens), BF16),
                pltpu.VMEM((2, rows), F32),
                pltpu.VMEM((heads + 1, inner, rows, depth), BF16),
                pltpu.VMEM((heads + 1, inner, 2, rows), F32),
                pltpu.VMEM((heads + 1, outer, rows, depth), BF16),
                pltpu.VMEM((heads + 1, outer, 2, rows), F32),
                pltpu.SemaphoreType.DMA((SLOTS,)),
                pltpu.SemaphoreType.DMA((SLOTS,)),
                pltpu.SemaphoreType.DMA((heads,)),
                pltpu.SemaphoreType.DMA((heads,)),
                pltpu.SemaphoreType.DMA((heads,)),
                pltpu.SemaphoreType.DMA((heads,)),
                pltpu.SemaphoreType.DMA((4,)),
            ],
            compiler_params=pltpu.CompilerParams(collective_id=0, has_side_effects=True, vmem_limit_bytes=56 * 2**20),
            name="attend",
        )(q, k, v)
        return out.transpose(1, 0, 2)

    return jax.shard_map(
        step,
        mesh=mesh,
        in_specs=(P("dp", None, None), P("dp", "sp", None, None), P("dp", "sp", None, None)),
        out_specs=P("dp", None, None),
        check_vma=False,
    )
```

time: 152 us -> 47.9 us (0.32)
  waiting for transfers between devices: 81.6 us -> 0 us
  Pallas kernels: 0 us -> 46.2 us
  matrix products: 32.6 us -> 0 us
  other arithmetic: 23.7 us -> 0 us
  between operations: 13.5 us -> 0.01 us
    all_gather x1 -> x0, waiting for transfers between devices: 81.5 us -> none  [step(): return together(lax.all_gather(part_of(q, k, v), 'sp')).reshape(q.shape)]
    pallas_call x0 -> x1, Pallas kernels: none -> 46.2 us  [step(): pl.pallas_call(functools.partial(kernel, n, inner), out_shape=jax.ShapeDt...]
    dot_general x2 -> x0, matrix products: 32.6 us -> none  [einsum(): return jnp.einsum(form, a.astype(jnp.float32), b.astype(jnp.float32))]
    reduce_sum x2 -> x0, other arithmetic: 14.3 us -> none  [the longest x1 11.1 us: together(): jnp.sum(total * scale, 0)]
    reduce_max x2 -> x0, other arithmetic: 7.25 us -> none  [the longest x1 7.03 us: together(): scale = jnp.exp(high - jnp.max(high, 0))]
    unnamed x2 -> x1, local copies, waits for them, and re-layouts: 0.01 us -> 1.59 us
  transfers between devices with their start and end apart: 1 -> 0, of which waited for: 1 -> 0; matrix products, arithmetic and copies ran while one was open for 0% -> 0% of each run, Pallas kernels for 0% -> 0%
where the time goes in v1:
time: 47.9 us; the launch traced here: 47.8 us
  Pallas kernels  46.2 us (96%)
  local copies, waits for them, and re-layouts  1.59 us (3%)
    pallas_call x1, Pallas kernels, step(): pl.pallas_call(functools.partial(kernel, n, inner), out_shape=jax.ShapeDt...  46.2 us
    unnamed x1, local copies, waits for them, and re-layouts  1.59 us

profile of v1, /device:TPU:97, one launch (start us, length us, event | category | flops | bytes accessed | tf_op | source)
XLA Modules:
  0.0 47.8 jit_solution(9570760286986913506)
XLA Ops:
  0.0 46.2 %attend.1 = bf16[20,32,128]{2,1,0:T(8,128)(2,1)} custom-call(bf16[20,32,128]{2,1,0:T(8,128)(2,1)} %bitcast.7, bf16[32,20,256,128]{3,2,1,0:T(8,128)(2,1)} %bitcast.4, bf16[32,20,256,128]{3,2,1,0:T(8,128)(2,1)} %bitcast.5), custom_call_target="tpu_custom_call" | custom-call | tf_op jit(solution)/shard_map/attend/pallas_call | solution.py:218
  46.2 1.6 %copy.5 = bf16[32,20,128]{2,0,1:T(8,128)(2,1)} copy(bf16[32,20,128]{2,0,1:T(8,128)(2,1)} %bitcast.6) | data formatting | bytes 327680

commit v2 on v0

v2 whole, which is shorter than its diff:
```python
import functools
import math

import jax
import jax.numpy as jnp
from jax import lax
from jax.experimental import pallas as pl
from jax.experimental.pallas import tpu as pltpu
from jax.sharding import PartitionSpec as P

SLOTS = 16
GROUP = 2
CHUNK = 8
BULK = 4
TAIL = 2
LAG = 3
F32, BF16 = jnp.float32, jnp.bfloat16


def scores_of(q, keys, slot):
    rows, depth = q.shape
    half, tokens = rows // 2, keys.shape[2]
    zero = jnp.zeros((half, depth), q.dtype)
    both = jnp.concatenate([jnp.concatenate([q[:half], zero], 1), jnp.concatenate([zero, q[half:]], 1)], 0)
    lane = lax.broadcasted_iota(jnp.int32, (tokens, rows), 1) % half
    scores = jnp.zeros((tokens, rows), F32)
    for pair in range(half):
        two = jnp.concatenate([keys[slot, pair], keys[slot, pair + half]], 1)
        got = lax.dot_general(two, both, (((1,), (1,)), ((), ())), preferred_element_type=F32)
        scores = jnp.where(lane == pair, got, scores)
    return scores


def seen_of(weights, values, slot, first):
    row = lax.broadcasted_iota(jnp.int32, (weights.shape[0], values.shape[3]), 0)
    out = jnp.zeros(row.shape, F32)
    for j in range(weights.shape[0]):
        out = jnp.where(row == j, jnp.dot(weights, values[slot, first + j], preferred_element_type=F32), out)
    return out


def kernel(n, inner, q_ref, k_ref, v_ref, o_ref, ring, scores, weights, stats, share, mine, parts_a, parts_b, last_mine, last_a, last_b, ring_sem, recv_s, recv_a, recv_b, recv_la, recv_lb, sent):
    heads, rows, depth = q_ref.shape
    half, outer = rows // 2, n // inner
    bulks = heads // BULK - 1
    first_last = bulks * BULK
    per = CHUNK // GROUP
    scale = depth**-0.5
    me = lax.axis_index("sp")
    core = lax.rem(me, 2)
    mine_a, mine_b = lax.rem(me, inner), me // inner * 2 + core
    base_a, base_b = me // inner * inner, lax.rem(me, inner) // 2 * 2
    peers_s = [lax.rem(me + i, n) for i in range(1, n)]
    peers_a = [base_a + lax.rem(mine_a + i, inner) for i in range(1, inner)]
    places_b = [lax.rem(mine_b + i, 2 * outer) for i in range(1, 2 * outer)]
    peers_b = [place // 2 * inner + base_b + lax.rem(place, 2) for place in places_b]

    def fetch(ref, head, place):
        slot = lax.rem(place, SLOTS)
        return [
            pltpu.make_async_copy(ref.at[pl.ds(h * half, half), head], ring.at[slot, pl.ds(h * half, half)], ring_sem.at[slot, h])
            for h in range(2)
        ]

    def fetch_k(head):
        return fetch(k_ref, head, head)

    def fetch_v(head):
        return fetch(v_ref, head, heads + head)

    def fetch_next(place, count):
        @pl.when(place < heads)
        def _():
            for g in range(count):
                for copy in fetch_k(place + g):
                    copy.start()

        @pl.when((place >= heads) & (place < 2 * heads))
        def _():
            for g in range(count):
                for copy in fetch_v(place + g - heads):
                    copy.start()

    def wait(copies):
        for copy in copies:
            copy.wait()

    for head in range(SLOTS):
        for copy in fetch_k(head):
            copy.start()
    stats[...] = jnp.zeros(stats.shape, stats.dtype)
    parts_a[bulks] = jnp.zeros(parts_a.shape[1:], parts_a.dtype)

    barrier = pltpu.get_barrier_semaphore()
    for peer in peers_s:
        pl.semaphore_signal(barrier, inc=1, device_id={"sp": peer}, device_id_type=pl.DeviceIdType.MESH)

    def send(source, target, peer, recv, place):
        pltpu.make_async_remote_copy(
            src_ref=source, dst_ref=target, send_sem=sent.at[place], recv_sem=recv, device_id={"sp": peer}, device_id_type=pl.DeviceIdType.MESH
        ).start()

    def arrived(ref, index, recv):
        some = ref.at[index, 0 : ref.shape[1] - 1]
        pltpu.make_async_copy(some, some, recv.at[index]).wait()

    def send_s(chunk):
        for peer in peers_s:
            send(stats.at[chunk, me], stats.at[chunk, me], peer, recv_s.at[chunk], 0)

    def send_a(own, parts, group, recv, place):
        for i, peer in enumerate(peers_a):
            send(own.at[group, lax.rem(core + i + 1, 2)], parts.at[group, mine_a], peer, recv.at[group], place)

    def send_b(parts, group, recv, place):
        for peer in peers_b:
            send(parts.at[group, mine_b], parts.at[group, mine_b], peer, recv.at[group], place)

    def weigh(group):
        for g in range(GROUP):
            head = group * GROUP + g
            scaled = scores[g] * scale
            high = jnp.max(scaled, 0, keepdims=True)
            w = jnp.exp(scaled - high)
            weights[head] = w.T.astype(BF16)
            chunk, j = head // CHUNK, lax.rem(head, CHUNK)
            stats[chunk, me, 0, pl.ds(j, 1)] = high
            stats[chunk, me, 1, pl.ds(j, 1)] = jnp.sum(w, 0, keepdims=True)

    def score(group):
        new = []
        for g in range(GROUP):
            head = group * GROUP + g
            new.append(scores_of(q_ref[head], ring, lax.rem(head, SLOTS)))
        for g in range(GROUP):
            scores[g] = new[g]

    def shares(chunk):
        top = stats[chunk, 0, 0]
        for j in range(1, n):
            top = jnp.maximum(top, stats[chunk, j, 0])
        total = stats[chunk, 0, 1] * jnp.exp(stats[chunk, 0, 0] - top)
        for j in range(1, n):
            total = total + stats[chunk, j, 1] * jnp.exp(stats[chunk, j, 0] - top)
        columns = (jnp.exp(stats[chunk, me, 0] - top) / total).T
        for j in range(CHUNK):
            share[chunk * CHUNK + j] = jnp.broadcast_to(columns[:, j : j + 1], (rows, depth))

    def part(own, parts, group, g, head, h):
        at = slice(h * half, (h + 1) * half)
        seen = (seen_of(weights[head, at], ring, lax.rem(heads + head, SLOTS), h * half) * share[head, at]).astype(BF16)
        own[group, h, g] = seen
        return seen

    def keep(parts, group, g, seen):
        parts[group, mine_a, g] = jnp.where(core == 0, seen[0], seen[1])

    def block(parts, to, group, to_group, count):
        for g in range(count):
            out = parts[group, 0, g].astype(F32)
            for j in range(1, inner):
                out = out + parts[group, j, g].astype(F32)
            to[to_group, mine_b, g] = out.astype(BF16)

    def final(parts, group, head, count):
        for g in range(count):
            for h in range(2):
                out = parts[group, h, g].astype(F32)
                for j in range(1, outer):
                    out = out + parts[group, 2 * j + h, g].astype(F32)
                o_ref[head + g, h * half : (h + 1) * half] = out.astype(o_ref.dtype)

    for g in range(GROUP):
        wait(fetch_k(g))
    score(0)
    fetch_next(SLOTS, GROUP)

    def keys_step(i, _):
        for g in range(GROUP):
            wait(fetch_k(i * GROUP + g))
        weigh(i - 1)
        score(i)
        fetch_next(i * GROUP + SLOTS, GROUP)

        @pl.when(i == per)
        def _():
            pl.semaphore_wait(barrier, n - 1)

        @pl.when(lax.rem(i, per) == 0)
        def _():
            send_s(i // per - 1)

        return 0

    lax.fori_loop(1, heads // GROUP, keys_step, 0)
    weigh(heads // GROUP - 1)
    send_s((heads - 1) // CHUNK)

    def values_step(i, _):
        a = i - LAG

        @pl.when(lax.rem(i, CHUNK // BULK) == 0)
        def _():
            arrived(stats, i // (CHUNK // BULK), recv_s)
            shares(i // (CHUNK // BULK))

        @pl.when(a >= 0)
        def _():
            arrived(parts_a, a, recv_a)

        for g in range(BULK):
            wait(fetch_v(i * BULK + g))
        for g in range(BULK):
            keep(parts_a, i, g, [part(mine, parts_a, i, g, i * BULK + g, h) for h in range(2)])
        block(parts_a, parts_b, jnp.where(a >= 0, a, bulks), jnp.where(a >= 0, a, bulks), BULK)
        send_a(mine, parts_a, i, recv_a, 1)

        @pl.when(a >= 0)
        def _():
            send_b(parts_b, a, recv_b, 2)

        fetch_next(heads + i * BULK + SLOTS, BULK)
        return 0

    lax.fori_loop(0, bulks, values_step, 0)

    def block_bulk(a):
        arrived(parts_a, a, recv_a)
        block(parts_a, parts_b, a, a, BULK)
        send_b(parts_b, a, recv_b, 2)

    def final_bulk(f):
        arrived(parts_b, f, recv_b)
        final(parts_b, f, f * BULK, BULK)

    arrived(stats, first_last // CHUNK, recv_s)
    shares(first_last // CHUNK)
    waiting = list(range(bulks - LAG, bulks))
    for t in range(BULK // TAIL):
        for g in range(TAIL):
            head = first_last + t * TAIL + g
            if head < heads - 1:
                wait(fetch_v(head))
            seen = []
            for h in range(2):
                if head == heads - 1:
                    fetch_v(head)[h].wait()
                seen.append(part(last_mine, last_a, t, g, head, h))
            keep(last_a, t, g, seen)
        send_a(last_mine, last_a, t, recv_la, 3)
        if t == 0:
            block_bulk(waiting.pop(0))
    for a in waiting:
        block_bulk(a)
    for f in range(bulks - LAG):
        final_bulk(f)
    for t in range(BULK // TAIL):
        arrived(last_a, t, recv_la)
        block(last_a, last_b, t, t, TAIL)
        send_b(last_b, t, recv_lb, 4)
    for f in range(bulks - LAG, bulks):
        final_bulk(f)
    for t in range(BULK // TAIL):
        arrived(last_b, t, recv_lb)
        final(last_b, t, first_last + t * TAIL, TAIL)
    every = (stats.at[:, 0 : n - 1], parts_a.at[0:bulks, 0 : inner - 1], parts_b.at[0:bulks, 0 : 2 * outer - 1], last_a.at[:, 0 : inner - 1], last_b.at[:, 0 : 2 * outer - 1])
    for place, some in enumerate(every):
        pltpu.make_async_copy(some, some, sent.at[place]).wait()


def solution(mesh):
    n = mesh.shape["sp"]
    inner = 2 * math.isqrt(n // 2)
    outer = n // inner

    def step(q, k, v):
        q, k, v = q.transpose(1, 0, 2), k.transpose(0, 2, 1, 3), v.transpose(0, 2, 1, 3)
        heads, rows, depth = q.shape
        tokens, half = k.shape[2], rows // 2
        chunks, bulks, lasts = -(-heads // CHUNK), heads // BULK - 1, BULK // TAIL
        whole = pl.BlockSpec(memory_space=pltpu.VMEM)
        out = pl.pallas_call(
            functools.partial(kernel, n, inner),
            out_shape=pltpu.VMEM(q.shape, q.dtype),
            in_specs=[whole, pl.BlockSpec(memory_space=pl.ANY), pl.BlockSpec(memory_space=pl.ANY)],
            out_specs=whole,
            scratch_shapes=[
                pltpu.VMEM((SLOTS, rows, tokens, depth), k.dtype),
                pltpu.VMEM((GROUP, tokens, rows), F32),
                pltpu.VMEM((heads, rows, tokens), BF16),
                pltpu.VMEM((chunks, n, 2, CHUNK, rows), F32),
                pltpu.VMEM((chunks * CHUNK, rows, depth), F32),
                pltpu.VMEM((bulks, 2, BULK, half, depth), BF16),
                pltpu.VMEM((bulks + 1, inner, BULK, half, depth), BF16),
                pltpu.VMEM((bulks + 1, 2 * outer, BULK, half, depth), BF16),
                pltpu.VMEM((lasts, 2, TAIL, half, depth), BF16),
                pltpu.VMEM((lasts, inner, TAIL, half, depth), BF16),
                pltpu.VMEM((lasts, 2 * outer, TAIL, half, depth), BF16),
                pltpu.SemaphoreType.DMA((SLOTS, 2)),
                pltpu.SemaphoreType.DMA((chunks,)),
                pltpu.SemaphoreType.DMA((bulks,)),
                pltpu.SemaphoreType.DMA((bulks,)),
                pltpu.SemaphoreType.DMA((lasts,)),
                pltpu.SemaphoreType.DMA((lasts,)),
                pltpu.SemaphoreType.DMA((5,)),
            ],
            compiler_params=pltpu.CompilerParams(collective_id=0, has_side_effects=True, vmem_limit_bytes=56 * 2**20),
            name="attend",
        )(q, k, v)
        return out.transpose(1, 0, 2)

    return jax.shard_map(
        step,
        mesh=mesh,
        in_specs=(P("dp", None, None), P("dp", "sp", None, None), P("dp", "sp", None, None)),
        out_specs=P("dp", None, None),
        check_vma=False,
    )
```

time: 152 us -> 41.9 us (0.28)
  waiting for transfers between devices: 81.6 us -> 0 us
  Pallas kernels: 0 us -> 41.1 us
  matrix products: 32.6 us -> 0 us
  other arithmetic: 23.7 us -> 0 us
  between operations: 13.5 us -> 0.01 us
    all_gather x1 -> x0, waiting for transfers between devices: 81.5 us -> none  [step(): return together(lax.all_gather(part_of(q, k, v), 'sp')).reshape(q.shape)]
    pallas_call x0 -> x1, Pallas kernels: none -> 41.1 us  [step(): pl.pallas_call(functools.partial(kernel, n, inner), out_shape=pltpu.VMEM(...]
    dot_general x2 -> x0, matrix products: 32.6 us -> none  [einsum(): return jnp.einsum(form, a.astype(jnp.float32), b.astype(jnp.float32))]
    reduce_sum x2 -> x0, other arithmetic: 14.3 us -> none  [the longest x1 11.1 us: together(): jnp.sum(total * scale, 0)]
    reduce_max x2 -> x0, other arithmetic: 7.25 us -> none  [the longest x1 7.03 us: together(): scale = jnp.exp(high - jnp.max(high, 0))]
  transfers between devices with their start and end apart: 1 -> 0, of which waited for: 1 -> 0; matrix products, arithmetic and copies ran while one was open for 0% -> 0% of each run, Pallas kernels for 0% -> 0%
where the time goes in v2:
time: 41.9 us; the launch traced here: 41.8 us
  Pallas kernels  41.1 us (98%)
  local copies, waits for them, and re-layouts  0.67 us (2%)
    pallas_call x1, Pallas kernels, step(): pl.pallas_call(functools.partial(kernel, n, inner), out_shape=pltpu.VMEM(...  41.1 us

profile of v2, /device:TPU:97, one launch (start us, length us, event | category | flops | bytes accessed | tf_op | source)
XLA Modules:
  0.0 41.8 jit_solution(2830873399869728767)
XLA Ops:
  0.0 41.1 %attend.1 = bf16[20,32,128]{2,1,0:T(8,128)(2,1)S(1)} custom-call(bf16[20,32,128]{2,1,0:T(8,128)(2,1)} %bitcast.7, bf16[32,20,256,128]{3,2,1,0:T(8,128)(2,1)} %bitcast.5, bf16[32,20,256,128]{3,2,1,0:T(8,128)(2,1)} %bitcast.6), custom_call_target="tpu_custom_call" | custom-call | tf_op jit(solution)/shard_map/attend/pallas_call | solution.py:282
  41.1 0.7 %copy.5 = bf16[32,20,128]{2,0,1:T(8,128)(2,1)} copy(bf16[32,20,128]{2,0,1:T(8,128)(2,1)S(1)} %bitcast.4) | data formatting | bytes 327680

commit v3 on v2

--- a/solution.py
+++ b/solution.py
@@ -13,6 +13,7 @@
 CHUNK = 8
 BULK = 4
 TAIL = 2
+PIECES = 2
 LAG = 3
 F32, BF16 = jnp.float32, jnp.bfloat16
 
@@ -31,17 +32,18 @@
     return scores
 
 
-def seen_of(weights, values, slot, first):
+def seen_of(weights, values, slot, first, ready):
     row = lax.broadcasted_iota(jnp.int32, (weights.shape[0], values.shape[3]), 0)
     out = jnp.zeros(row.shape, F32)
     for j in range(weights.shape[0]):
+        ready(first + j)
         out = jnp.where(row == j, jnp.dot(weights, values[slot, first + j], preferred_element_type=F32), out)
     return out
 
 
-def kernel(n, inner, q_ref, k_ref, v_ref, o_ref, ring, scores, weights, stats, share, mine, parts_a, parts_b, last_mine, last_a, last_b, ring_sem, recv_s, recv_a, recv_b, recv_la, recv_lb, sent):
+def kernel(n, inner, q_hbm, k_ref, v_ref, o_ref, q_ref, ring, scores, weights, stats, share, mine, parts_a, parts_b, last_mine, last_a, last_b, q_sem, ring_sem, recv_s, recv_a, recv_b, recv_la, recv_lb, sent):
     heads, rows, depth = q_ref.shape
-    half, outer = rows // 2, n // inner
+    half, outer, piece = rows // 2, n // inner, rows // PIECES
     bulks = heads // BULK - 1
     first_last = bulks * BULK
     per = CHUNK // GROUP
@@ -50,16 +52,19 @@
     core = lax.rem(me, 2)
     mine_a, mine_b = lax.rem(me, inner), me // inner * 2 + core
     base_a, base_b = me // inner * inner, lax.rem(me, inner) // 2 * 2
+    def far_first(count):
+        return sorted(range(1, count), key=lambda i: -min(i, count - i))
+
     peers_s = [lax.rem(me + i, n) for i in range(1, n)]
-    peers_a = [base_a + lax.rem(mine_a + i, inner) for i in range(1, inner)]
-    places_b = [lax.rem(mine_b + i, 2 * outer) for i in range(1, 2 * outer)]
+    peers_a = [(i, base_a + lax.rem(mine_a + i, inner)) for i in far_first(inner)]
+    places_b = [lax.rem(mine_b + i, 2 * outer) for i in far_first(2 * outer)]
     peers_b = [place // 2 * inner + base_b + lax.rem(place, 2) for place in places_b]
 
     def fetch(ref, head, place):
         slot = lax.rem(place, SLOTS)
         return [
-            pltpu.make_async_copy(ref.at[pl.ds(h * half, half), head], ring.at[slot, pl.ds(h * half, half)], ring_sem.at[slot, h])
-            for h in range(2)
+            pltpu.make_async_copy(ref.at[pl.ds(p * piece, piece), head], ring.at[slot, pl.ds(p * piece, piece)], ring_sem.at[slot, p])
+            for p in range(PIECES)
         ]
 
     def fetch_k(head):
@@ -85,7 +90,9 @@
         for copy in copies:
             copy.wait()
 
-    for head in range(SLOTS):
+    fetch_q = pltpu.make_async_copy(q_hbm, q_ref, q_sem)
+    fetch_q.start()
+    for head in range(GROUP):
         for copy in fetch_k(head):
             copy.start()
     stats[...] = jnp.zeros(stats.shape, stats.dtype)
@@ -94,6 +101,9 @@
     barrier = pltpu.get_barrier_semaphore()
     for peer in peers_s:
         pl.semaphore_signal(barrier, inc=1, device_id={"sp": peer}, device_id_type=pl.DeviceIdType.MESH)
+    for head in range(GROUP, SLOTS):
+        for copy in fetch_k(head):
+            copy.start()
 
     def send(source, target, peer, recv, place):
         pltpu.make_async_remote_copy(
@@ -109,8 +119,8 @@
             send(stats.at[chunk, me], stats.at[chunk, me], peer, recv_s.at[chunk], 0)
 
     def send_a(own, parts, group, recv, place):
-        for i, peer in enumerate(peers_a):
-            send(own.at[group, lax.rem(core + i + 1, 2)], parts.at[group, mine_a], peer, recv.at[group], place)
+        for i, peer in peers_a:
+            send(own.at[group, lax.rem(core + i, 2)], parts.at[group, mine_a], peer, recv.at[group], place)
 
     def send_b(parts, group, recv, place):
         for peer in peers_b:
@@ -146,9 +156,9 @@
         for j in range(CHUNK):
             share[chunk * CHUNK + j] = jnp.broadcast_to(columns[:, j : j + 1], (rows, depth))
 
-    def part(own, parts, group, g, head, h):
+    def part(own, group, g, head, h, ready=lambda row: None):
         at = slice(h * half, (h + 1) * half)
-        seen = (seen_of(weights[head, at], ring, lax.rem(heads + head, SLOTS), h * half) * share[head, at]).astype(BF16)
+        seen = (seen_of(weights[head, at], ring, lax.rem(heads + head, SLOTS), h * half, ready) * share[head, at]).astype(BF16)
         own[group, h, g] = seen
         return seen
 
@@ -170,6 +180,7 @@
                     out = out + parts[group, 2 * j + h, g].astype(F32)
                 o_ref[head + g, h * half : (h + 1) * half] = out.astype(o_ref.dtype)
 
+    fetch_q.wait()
     for g in range(GROUP):
         wait(fetch_k(g))
     score(0)
@@ -211,7 +222,7 @@
         for g in range(BULK):
             wait(fetch_v(i * BULK + g))
         for g in range(BULK):
-            keep(parts_a, i, g, [part(mine, parts_a, i, g, i * BULK + g, h) for h in range(2)])
+            keep(parts_a, i, g, [part(mine, i, g, i * BULK + g, h) for h in range(2)])
         block(parts_a, parts_b, jnp.where(a >= 0, a, bulks), jnp.where(a >= 0, a, bulks), BULK)
         send_a(mine, parts_a, i, recv_a, 1)
 
@@ -239,14 +250,15 @@
     for t in range(BULK // TAIL):
         for g in range(TAIL):
             head = first_last + t * TAIL + g
+            copies = fetch_v(head)
             if head < heads - 1:
-                wait(fetch_v(head))
-            seen = []
-            for h in range(2):
-                if head == heads - 1:
-                    fetch_v(head)[h].wait()
-                seen.append(part(last_mine, last_a, t, g, head, h))
-            keep(last_a, t, g, seen)
+                wait(copies)
+
+            def ready(row):
+                if head == heads - 1 and row % piece == 0:
+                    copies[row // piece].wait()
+
+            keep(last_a, t, g, [part(last_mine, t, g, head, h, ready) for h in range(2)])
         send_a(last_mine, last_a, t, recv_la, 3)
         if t == 0:
             block_bulk(waiting.pop(0))
@@ -282,9 +294,10 @@
         out = pl.pallas_call(
             functools.partial(kernel, n, inner),
             out_shape=pltpu.VMEM(q.shape, q.dtype),
-            in_specs=[whole, pl.BlockSpec(memory_space=pl.ANY), pl.BlockSpec(memory_space=pl.ANY)],
+            in_specs=[pl.BlockSpec(memory_space=pl.ANY)] * 3,
             out_specs=whole,
             scratch_shapes=[
+                pltpu.VMEM(q.shape, q.dtype),
                 pltpu.VMEM((SLOTS, rows, tokens, depth), k.dtype),
                 pltpu.VMEM((GROUP, tokens, rows), F32),
                 pltpu.VMEM((heads, rows, tokens), BF16),
@@ -296,7 +309,8 @@
                 pltpu.VMEM((lasts, 2, TAIL, half, depth), BF16),
                 pltpu.VMEM((lasts, inner, TAIL, half, depth), BF16),
                 pltpu.VMEM((lasts, 2 * outer, TAIL, half, depth), BF16),
-                pltpu.SemaphoreType.DMA((SLOTS, 2)),
+                pltpu.SemaphoreType.DMA,
+                pltpu.SemaphoreType.DMA((SLOTS, PIECES)),
                 pltpu.SemaphoreType.DMA((chunks,)),
                 pltpu.SemaphoreType.DMA((bulks,)),
                 pltpu.SemaphoreType.DMA((bulks,)),

time: 41.9 us -> 40.5 us (0.967)
  Pallas kernels: 41.1 us -> 39.7 us
    pallas_call x1, Pallas kernels: 41.1 us -> 39.7 us  [step(): pl.pallas_call(functools.partial(kernel, n, inner), out_shape=pltpu.VMEM(...]
where the time goes in v3:
time: 40.5 us; the launch traced here: 40.4 us
  Pallas kernels  39.7 us (98%)
  local copies, waits for them, and re-layouts  0.67 us (2%)
    pallas_call x1, Pallas kernels, step(): pl.pallas_call(functools.partial(kernel, n, inner), out_shape=pltpu.VMEM(...  39.7 us

profile of v3, /device:TPU:97, one launch (start us, length us, event | category | flops | bytes accessed | tf_op | source)
XLA Modules:
  0.0 40.4 jit_solution(3495588711383032682)
XLA Ops:
  0.0 39.7 %attend.1 = bf16[20,32,128]{2,1,0:T(8,128)(2,1)S(1)} custom-call(bf16[20,32,128]{2,1,0:T(8,128)(2,1)} %bitcast.7, bf16[32,20,256,128]{3,2,1,0:T(8,128)(2,1)} %bitcast.5, bf16[32,20,256,128]{3,2,1,0:T(8,128)(2,1)} %bitcast.6), custom_call_target="tpu_custom_call" | custom-call | tf_op jit(solution)/shard_map/attend/pallas_call | solution.py:294
  39.7 0.7 %copy.5 = bf16[32,20,128]{2,0,1:T(8,128)(2,1)} copy(bf16[32,20,128]{2,0,1:T(8,128)(2,1)S(1)} %bitcast.4) | data formatting | bytes 327680

commit v4 on v3

--- a/solution.py
+++ b/solution.py
@@ -13,8 +13,8 @@
 CHUNK = 8
 BULK = 4
 TAIL = 2
+LAST = 8
 PIECES = 2
-LAG = 3
 F32, BF16 = jnp.float32, jnp.bfloat16
 
 
@@ -44,7 +44,7 @@
 def kernel(n, inner, q_hbm, k_ref, v_ref, o_ref, q_ref, ring, scores, weights, stats, share, mine, parts_a, parts_b, last_mine, last_a, last_b, q_sem, ring_sem, recv_s, recv_a, recv_b, recv_la, recv_lb, sent):
     heads, rows, depth = q_ref.shape
     half, outer, piece = rows // 2, n // inner, rows // PIECES
-    bulks = heads // BULK - 1
+    bulks, lasts = (heads - LAST) // BULK, LAST // TAIL
     first_last = bulks * BULK
     per = CHUNK // GROUP
     scale = depth**-0.5
@@ -53,7 +53,7 @@
     mine_a, mine_b = lax.rem(me, inner), me // inner * 2 + core
     base_a, base_b = me // inner * inner, lax.rem(me, inner) // 2 * 2
     def far_first(count):
-        return sorted(range(1, count), key=lambda i: -min(i, count - i))
+        return sorted(range(1, count), key=lambda i: -min(i // 2 * 2, count - i // 2 * 2))
 
     peers_s = [lax.rem(me + i, n) for i in range(1, n)]
     peers_a = [(i, base_a + lax.rem(mine_a + i, inner)) for i in far_first(inner)]
@@ -96,7 +96,6 @@
         for copy in fetch_k(head):
             copy.start()
     stats[...] = jnp.zeros(stats.shape, stats.dtype)
-    parts_a[bulks] = jnp.zeros(parts_a.shape[1:], parts_a.dtype)
 
     barrier = pltpu.get_barrier_semaphore()
     for peer in peers_s:
@@ -134,8 +133,7 @@
             w = jnp.exp(scaled - high)
             weights[head] = w.T.astype(BF16)
             chunk, j = head // CHUNK, lax.rem(head, CHUNK)
-            stats[chunk, me, 0, pl.ds(j, 1)] = high
-            stats[chunk, me, 1, pl.ds(j, 1)] = jnp.sum(w, 0, keepdims=True)
+            stats[chunk, me, pl.ds(j, 1)] = jnp.concatenate([high, jnp.sum(w, 0, keepdims=True)], 1)
 
     def score(group):
         new = []
@@ -146,13 +144,13 @@
             scores[g] = new[g]
 
     def shares(chunk):
-        top = stats[chunk, 0, 0]
+        top = stats[chunk, 0, :, :rows]
         for j in range(1, n):
-            top = jnp.maximum(top, stats[chunk, j, 0])
-        total = stats[chunk, 0, 1] * jnp.exp(stats[chunk, 0, 0] - top)
-        for j in range(1, n):
-            total = total + stats[chunk, j, 1] * jnp.exp(stats[chunk, j, 0] - top)
-        columns = (jnp.exp(stats[chunk, me, 0] - top) / total).T
+            top = jnp.maximum(top, stats[chunk, j, :, :rows])
+        total = jnp.zeros(top.shape, F32)
+        for j in range(n):
+            total = total + stats[chunk, j, :, rows:] * jnp.exp(stats[chunk, j, :, :rows] - top)
+        columns = (jnp.exp(stats[chunk, me, :, :rows] - top) / total).T
         for j in range(CHUNK):
             share[chunk * CHUNK + j] = jnp.broadcast_to(columns[:, j : j + 1], (rows, depth))
 
@@ -207,29 +205,20 @@
     weigh(heads // GROUP - 1)
     send_s((heads - 1) // CHUNK)
 
+    def ready_s(head):
+        arrived(stats, head // CHUNK, recv_s)
+        shares(head // CHUNK)
+
     def values_step(i, _):
-        a = i - LAG
-
         @pl.when(lax.rem(i, CHUNK // BULK) == 0)
         def _():
-            arrived(stats, i // (CHUNK // BULK), recv_s)
-            shares(i // (CHUNK // BULK))
-
-        @pl.when(a >= 0)
-        def _():
-            arrived(parts_a, a, recv_a)
+            ready_s(i * BULK)
 
         for g in range(BULK):
             wait(fetch_v(i * BULK + g))
         for g in range(BULK):
             keep(parts_a, i, g, [part(mine, i, g, i * BULK + g, h) for h in range(2)])
-        block(parts_a, parts_b, jnp.where(a >= 0, a, bulks), jnp.where(a >= 0, a, bulks), BULK)
         send_a(mine, parts_a, i, recv_a, 1)
-
-        @pl.when(a >= 0)
-        def _():
-            send_b(parts_b, a, recv_b, 2)
-
         fetch_next(heads + i * BULK + SLOTS, BULK)
         return 0
 
@@ -244,12 +233,20 @@
         arrived(parts_b, f, recv_b)
         final(parts_b, f, f * BULK, BULK)
 
-    arrived(stats, first_last // CHUNK, recv_s)
-    shares(first_last // CHUNK)
-    waiting = list(range(bulks - LAG, bulks))
-    for t in range(BULK // TAIL):
+    def block_last(t):
+        arrived(last_a, t, recv_la)
+        block(last_a, last_b, t, t, TAIL)
+        send_b(last_b, t, recv_lb, 4)
+
+    def final_last(t):
+        arrived(last_b, t, recv_lb)
+        final(last_b, t, first_last + t * TAIL, TAIL)
+
+    for t in range(lasts):
         for g in range(TAIL):
             head = first_last + t * TAIL + g
+            if head % CHUNK == 0:
+                ready_s(head)
             copies = fetch_v(head)
             if head < heads - 1:
                 wait(copies)
@@ -260,22 +257,17 @@
 
             keep(last_a, t, g, [part(last_mine, t, g, head, h, ready) for h in range(2)])
         send_a(last_mine, last_a, t, recv_la, 3)
-        if t == 0:
-            block_bulk(waiting.pop(0))
-    for a in waiting:
+        if t < bulks - 1:
+            block_bulk(t)
+    for a in range(min(lasts, bulks - 1), bulks):
         block_bulk(a)
-    for f in range(bulks - LAG):
+    for t in range(lasts):
+        block_last(t)
+    for f in range(bulks):
         final_bulk(f)
-    for t in range(BULK // TAIL):
-        arrived(last_a, t, recv_la)
-        block(last_a, last_b, t, t, TAIL)
-        send_b(last_b, t, recv_lb, 4)
-    for f in range(bulks - LAG, bulks):
-        final_bulk(f)
-    for t in range(BULK // TAIL):
-        arrived(last_b, t, recv_lb)
-        final(last_b, t, first_last + t * TAIL, TAIL)
-    every = (stats.at[:, 0 : n - 1], parts_a.at[0:bulks, 0 : inner - 1], parts_b.at[0:bulks, 0 : 2 * outer - 1], last_a.at[:, 0 : inner - 1], last_b.at[:, 0 : 2 * outer - 1])
+    for t in range(lasts):
+        final_last(t)
+    every = (stats.at[:, 0 : n - 1], parts_a.at[:, 0 : inner - 1], parts_b.at[:, 0 : 2 * outer - 1], last_a.at[:, 0 : inner - 1], last_b.at[:, 0 : 2 * outer - 1])
     for place, some in enumerate(every):
         pltpu.make_async_copy(some, some, sent.at[place]).wait()
 
@@ -289,7 +281,7 @@
         q, k, v = q.transpose(1, 0, 2), k.transpose(0, 2, 1, 3), v.transpose(0, 2, 1, 3)
         heads, rows, depth = q.shape
         tokens, half = k.shape[2], rows // 2
-        chunks, bulks, lasts = -(-heads // CHUNK), heads // BULK - 1, BULK // TAIL
+        chunks, bulks, lasts = -(-heads // CHUNK), (heads - LAST) // BULK, LAST // TAIL
         whole = pl.BlockSpec(memory_space=pltpu.VMEM)
         out = pl.pallas_call(
             functools.partial(kernel, n, inner),
@@ -301,11 +293,11 @@
                 pltpu.VMEM((SLOTS, rows, tokens, depth), k.dtype),
                 pltpu.VMEM((GROUP, tokens, rows), F32),
                 pltpu.VMEM((heads, rows, tokens), BF16),
-                pltpu.VMEM((chunks, n, 2, CHUNK, rows), F32),
+                pltpu.VMEM((chunks, n, CHUNK, 2 * rows), F32),
                 pltpu.VMEM((chunks * CHUNK, rows, depth), F32),
                 pltpu.VMEM((bulks, 2, BULK, half, depth), BF16),
-                pltpu.VMEM((bulks + 1, inner, BULK, half, depth), BF16),
-                pltpu.VMEM((bulks + 1, 2 * outer, BULK, half, depth), BF16),
+                pltpu.VMEM((bulks, inner, BULK, half, depth), BF16),
+                pltpu.VMEM((bulks, 2 * outer, BULK, half, depth), BF16),
                 pltpu.VMEM((lasts, 2, TAIL, half, depth), BF16),
                 pltpu.VMEM((lasts, inner, TAIL, half, depth), BF16),
                 pltpu.VMEM((lasts, 2 * outer, TAIL, half, depth), BF16),

time: 40.5 us -> 39.5 us (0.975)
  Pallas kernels: 39.7 us -> 38.8 us
    pallas_call x1, Pallas kernels: 39.7 us -> 38.8 us  [step(): pl.pallas_call(functools.partial(kernel, n, inner), out_shape=pltpu.VMEM(...]
where the time goes in v4:
time: 39.5 us
  Pallas kernels  38.8 us (98%)
  local copies, waits for them, and re-layouts  0.67 us (2%)
    pallas_call x1, Pallas kernels, step(): pl.pallas_call(functools.partial(kernel, n, inner), out_shape=pltpu.VMEM(...  38.8 us

profile of v4, /device:TPU:97, one launch (start us, length us, event | category | flops | bytes accessed | tf_op | source)
XLA Modules:
  0.0 39.5 jit_solution(4416716927690956448)
XLA Ops:
  0.0 38.8 %attend.1 = bf16[20,32,128]{2,1,0:T(8,128)(2,1)S(1)} custom-call(bf16[20,32,128]{2,1,0:T(8,128)(2,1)} %bitcast.7, bf16[32,20,256,128]{3,2,1,0:T(8,128)(2,1)} %bitcast.5, bf16[32,20,256,128]{3,2,1,0:T(8,128)(2,1)} %bitcast.6), custom_call_target="tpu_custom_call" | custom-call | tf_op jit(solution)/shard_map/attend/pallas_call | solution.py:286
  38.8 0.7 %copy.5 = bf16[32,20,128]{2,0,1:T(8,128)(2,1)} copy(bf16[32,20,128]{2,0,1:T(8,128)(2,1)S(1)} %bitcast.4) | data formatting | bytes 327680

commit v5 on v4

--- a/solution.py
+++ b/solution.py
@@ -32,11 +32,10 @@
     return scores
 
 
-def seen_of(weights, values, slot, first, ready):
+def seen_of(weights, values, slot, first):
     row = lax.broadcasted_iota(jnp.int32, (weights.shape[0], values.shape[3]), 0)
     out = jnp.zeros(row.shape, F32)
     for j in range(weights.shape[0]):
-        ready(first + j)
         out = jnp.where(row == j, jnp.dot(weights, values[slot, first + j], preferred_element_type=F32), out)
     return out
 
@@ -154,9 +153,9 @@
         for j in range(CHUNK):
             share[chunk * CHUNK + j] = jnp.broadcast_to(columns[:, j : j + 1], (rows, depth))
 
-    def part(own, group, g, head, h, ready=lambda row: None):
+    def part(own, group, g, head, h):
         at = slice(h * half, (h + 1) * half)
-        seen = (seen_of(weights[head, at], ring, lax.rem(heads + head, SLOTS), h * half, ready) * share[head, at]).astype(BF16)
+        seen = (seen_of(weights[head, at], ring, lax.rem(heads + head, SLOTS), h * half) * share[head, at]).astype(BF16)
         own[group, h, g] = seen
         return seen
 
@@ -247,15 +246,8 @@
             head = first_last + t * TAIL + g
             if head % CHUNK == 0:
                 ready_s(head)
-            copies = fetch_v(head)
-            if head < heads - 1:
-                wait(copies)
-
-            def ready(row):
-                if head == heads - 1 and row % piece == 0:
-                    copies[row // piece].wait()
-
-            keep(last_a, t, g, [part(last_mine, t, g, head, h, ready) for h in range(2)])
+            wait(fetch_v(head))
+            keep(last_a, t, g, [part(last_mine, t, g, head, h) for h in range(2)])
         send_a(last_mine, last_a, t, recv_la, 3)
         if t < bulks - 1:
             block_bulk(t)

time: 39.5 us -> 39.4 us (level)
  no operation moved by 1% of the time
where the time goes in v5:
time: 39.4 us
  Pallas kernels  38.7 us (98%)
  local copies, waits for them, and re-layouts  0.67 us (2%)
    pallas_call x1, Pallas kernels, step(): pl.pallas_call(functools.partial(kernel, n, inner), out_shape=pltpu.VMEM(...  38.7 us

profile of v5, /device:TPU:97, one launch (start us, length us, event | category | flops | bytes accessed | tf_op | source)
XLA Modules:
  0.0 39.4 jit_solution(5183830894339707912)
XLA Ops:
  0.0 38.7 %attend.1 = bf16[20,32,128]{2,1,0:T(8,128)(2,1)S(1)} custom-call(bf16[20,32,128]{2,1,0:T(8,128)(2,1)} %bitcast.7, bf16[32,20,256,128]{3,2,1,0:T(8,128)(2,1)} %bitcast.5, bf16[32,20,256,128]{3,2,1,0:T(8,128)(2,1)} %bitcast.6), custom_call_target="tpu_custom_call" | custom-call | tf_op jit(solution)/shard_map/attend/pallas_call | solution.py:278
  38.7 0.7 %copy.5 = bf16[32,20,128]{2,0,1:T(8,128)(2,1)} copy(bf16[32,20,128]{2,0,1:T(8,128)(2,1)S(1)} %bitcast.4) | data formatting | bytes 327680
